TPU v7x, 32 devices: a whole 2x2x4 slice. The times are simulated.
32 devices in a mesh: dp: 8 (over z, x), mp: 4 (over y, core).
Axes of the slice: x: 2, y: 2, z: 4, core: 2. Of those that a mesh axis runs over, the one named last changes fastest.
Arguments:
- hidden: bfloat16 [16, 4608], P('dp'), may hold values from -6 to 6
- in_gain: float32 [1, 4608], replicated, may hold values from 0.5 to 1.5
- post_gain: float32 [1, 4608], replicated, may hold values from 0.5 to 1.5
- query_weight: bfloat16 [1, 4608, 2048], P(None, 'dp', 'mp'), may hold values from -0.09375 to 0.09375
- key_weight: bfloat16 [1, 4608, 1024], P(None, 'dp', 'mp'), may hold values from -0.09375 to 0.09375
- value_weight: bfloat16 [1, 4608, 1024], P(None, 'dp', 'mp'), may hold values from -0.09375 to 0.09375
- out_weight: bfloat16 [1, 2048, 4608], P(None, 'mp', 'dp'), may hold values from -0.125 to 0.125
- key_cache: bfloat16 [1, 16, 512, 8, 128], P(None, 'dp', 'mp'), may hold values from -6 to 6
- value_cache: bfloat16 [1, 16, 512, 8, 128], P(None, 'dp', 'mp'), may hold values from -6 to 6
- lengths: int32 [16], P('dp'), may hold values from 256 to 512
- windowed: int32 [1, 16], P(None, 'dp'), may hold values from 0 to 1
Outputs:
- hidden_out: bfloat16 [16, 4608], P('dp')
- new_keys: bfloat16 [1, 16, 8, 128], P(None, 'dp')
- new_values: bfloat16 [1, 16, 8, 128], P(None, 'dp')
Inputs may be any that keep to these rules, and one draw needn't show every extreme that they name: `lengths`: every request has between 256 and 512 cached tokens. `windowed`: each flag is 0 or 1, for every layer and request.
All inputs are finite; a program needn't handle non-finite values.
Results may differ from a plain program's by a relative error of at most 0.008.
Values may be sent and summed in bfloat16 or wider, within the bound.
A program may use at most 64 MiB of HBM per device.

v0:
```python
import jax
import jax.numpy as jnp
from jax import lax
from jax.sharding import PartitionSpec as P

HEADS = 16
KV_HEADS = 8
HEAD_DIM = 128
LAYERS = 1
EPSILON = 1e-06
SOFTCAP = 50.0
ROPE_BASE = 10000.0
NEGATIVE = -1e30


def rms_scale(values, gain_row):
    values = values.astype(jnp.float32)
    mean_square = jnp.mean(values * values, axis=-1, keepdims=True)
    return values * lax.rsqrt(mean_square + EPSILON) * gain_row.astype(jnp.float32)


def rotate(values, positions):
    half_dim = values.shape[-1] // 2
    frequency = jnp.power(
        ROPE_BASE, -2.0 * jnp.arange(half_dim, dtype=jnp.float32) / values.shape[-1]
    )
    angles = positions.astype(jnp.float32)[:, None] * frequency[None, :]
    cosine = jnp.cos(angles)[:, None, :]
    sine_table = jnp.sin(angles)[:, None, :]
    front_half = values[..., :half_dim]
    back_half = values[..., half_dim:]
    return jnp.concatenate(
        (
            front_half * cosine - back_half * sine_table,
            back_half * cosine + front_half * sine_table,
        ),
        axis=-1,
    )


def on_device(
    hidden,
    in_gain,
    post_gain,
    query_weight,
    key_weight,
    value_weight,
    out_weight,
    key_cache,
    value_cache,
    lengths,
    windowed,
):
    row_count = hidden.shape[0]
    query_width = query_weight.shape[2]
    key_width = key_weight.shape[2]
    seq_block = key_cache.shape[2]
    head_width = out_weight.shape[1]
    group_size = HEADS // KV_HEADS
    window_len = seq_block * lax.axis_size("mp") // 2
    keys_out = []
    values_out = []
    for layer_index in range(LAYERS):
        normed = rms_scale(hidden, in_gain[layer_index]).astype(jnp.bfloat16)
        token_slab = lax.all_to_all(normed, "dp", split_axis=1, concat_axis=0, tiled=True)
        joined = jnp.concatenate(
            (query_weight[layer_index], key_weight[layer_index], value_weight[layer_index]), 1
        )

        def local_term():
            part_rows = lax.slice_in_dim(token_slab, 0, row_count * lax.axis_size("dp"), axis=0)
            return jnp.dot(part_rows, joined, preferred_element_type=jnp.float32)

        summed = lax.psum_scatter(local_term(), "dp", scatter_dimension=0, tiled=True)
        query_part = summed[:, :query_width]
        key_part = summed[:, query_width : query_width + key_width]
        value_part = summed[:, query_width + key_width :]
        rounded = (
            query_part.astype(jnp.bfloat16),
            key_part.astype(jnp.bfloat16),
            value_part.astype(jnp.bfloat16),
        )
        query, key_raw, value_new = (
            lax.all_gather(rounded[0], "mp", axis=1, tiled=True),
            lax.all_gather(rounded[1], "mp", axis=1, tiled=True),
            lax.all_gather(rounded[2], "mp", axis=1, tiled=True),
        )
        queries = rotate(query.astype(jnp.float32).reshape(row_count, HEADS, HEAD_DIM), lengths)
        queries = (queries * HEAD_DIM ** (-0.5)).astype(jnp.bfloat16)
        keys_new = rotate(
            key_raw.astype(jnp.float32).reshape(row_count, KV_HEADS, HEAD_DIM), lengths
        ).astype(jnp.bfloat16)
        value_new = value_new.reshape(row_count, KV_HEADS, HEAD_DIM)
        grouped = queries.reshape(row_count, KV_HEADS, group_size, HEAD_DIM)
        scores = jnp.einsum(
            "rkgd,rskd->rkgs", grouped, key_cache[layer_index], preferred_element_type=jnp.float32
        )
        scores = SOFTCAP * jnp.tanh(scores / SOFTCAP)
        positions = lax.axis_index("mp") * seq_block + jnp.arange(seq_block, dtype=jnp.int32)
        window_flag = windowed[layer_index][:, None]
        usable = (positions[None, :] < lengths[:, None]) & (
            (window_flag == 0) | (positions[None, :] > lengths[:, None] - window_len)
        )
        usable = usable[:, None, None, :]
        masked = jnp.where(usable, scores, NEGATIVE)
        peaks = jnp.max(masked, axis=-1)
        exp_scores = jnp.where(usable, jnp.exp(masked - peaks[..., None]), 0.0)
        sums_exp = jnp.sum(exp_scores, axis=-1)
        accumulated = jnp.einsum(
            "rkgs,rskd->rkgd",
            exp_scores,
            value_cache[layer_index].astype(jnp.float32),
            preferred_element_type=jnp.float32,
        )
        global_peak = lax.pmax(peaks, "mp")
        rescale = jnp.exp(peaks - global_peak)
        sums_exp, accumulated = lax.psum(
            (sums_exp * rescale, accumulated * rescale[..., None]), "mp"
        )
        peaks = global_peak
        self_score = jnp.einsum(
            "rkgd,rkd->rkg", grouped, keys_new, preferred_element_type=jnp.float32
        )
        self_score = SOFTCAP * jnp.tanh(self_score / SOFTCAP)
        peak_all = jnp.maximum(peaks, self_score)
        old_scale = jnp.exp(peaks - peak_all)
        self_weight = jnp.exp(self_score - peak_all)
        denominator = sums_exp * old_scale + self_weight
        mixed = (
            accumulated * old_scale[..., None]
            + self_weight[..., None] * value_new.astype(jnp.float32)[:, :, None, :]
        )
        attended = (
            (mixed / denominator[..., None])
            .reshape(row_count, HEADS * HEAD_DIM)
            .astype(jnp.bfloat16)
        )
        attended_local = lax.dynamic_slice_in_dim(
            attended, lax.axis_index("mp") * head_width, head_width, 1
        )
        all_rows = lax.all_gather(attended_local, "dp", axis=0, tiled=True)
        partial_cols = jnp.dot(
            all_rows, out_weight[layer_index], preferred_element_type=jnp.float32
        )
        partial_cols = lax.psum(partial_cols, "mp")
        projected = lax.all_to_all(partial_cols, "dp", split_axis=0, concat_axis=1, tiled=True)
        hidden = (hidden.astype(jnp.float32) + rms_scale(projected, post_gain[layer_index])).astype(
            jnp.bfloat16
        )
        keys_out.append(keys_new)
        values_out.append(value_new)
    return (hidden, jnp.stack(keys_out), jnp.stack(values_out))


def solution(mesh):
    return jax.shard_map(
        on_device,
        mesh=mesh,
        in_specs=(
            P("dp", None),
            P(),
            P(),
            P(None, "dp", "mp"),
            P(None, "dp", "mp"),
            P(None, "dp", "mp"),
            P(None, "mp", "dp"),
            P(None, "dp", "mp", None, None),
            P(None, "dp", "mp", None, None),
            P("dp"),
            P(None, "dp"),
        ),
        out_specs=(P("dp", None), P(None, "dp", None, None), P(None, "dp", None, None)),
        check_vma=False,
    )
```

profile of v0, /device:TPU:0, one launch (start us, length us, event | category | flops | bytes accessed | tf_op | source)
XLA Modules:
  0.0 139.7 jit_solution(18006181525195604881)
XLA Ops:
  0.6 0.0 copy-start
  0.6 0.9 fusion.13
  1.6 0.8 reduce.1
  2.4 0.8 fusion.15
  3.2 0.1 all_to_all.28
  3.3 0.6 copy.21
  3.9 7.3 %all-to-all-start = ((bf16[2,8,576]{2,0,1:T(2,128)(2,1)}), bf16[2,8,576]{2,0,1:T(2,128)(2,1)S(1)}, u32[]{:S(2)}, u32[]{:S(2)}) async-start(bf16[2,8,576]{2,0,1:T(2,128)(2,1)} %copy.21), calls=%async_computation | async-start | bytes 40960 | tf_op jit(solution)/shard_map/all_to_all | solution.py:65
  11.2 0.7 compare_bitcast_fusion
  11.9 0.7 broadcast_add_fusion
  12.6 0.1 multiply_cosine_fusion
  12.7 0.7 or_and_fusion
  13.4 0.8 reduce.2
  14.2 1.2 dynamic-slice
  16.1 1.7 %all-to-all-done = bf16[2,8,576]{2,0,1:T(2,128)(2,1)S(1)} async-done(((bf16[2,8,576]{2,0,1:T(2,128)(2,1)}), bf16[2,8,576]{2,0,1:T(2,128)(2,1)S(1)}, u32[]{:S(2)}, u32[]{:S(2)}) %all-to-all-start) | async-done | bytes 18464 | tf_op jit(solution)/shard_map/all_to_all | solution.py:65
  17.8 0.0 copy-start.2
  17.8 1.6 %fusion = f32[16,1024]{1,0:T(8,128)S(1)} fusion(bf16[16,576]{1,0:T(8,128)(2,1)S(1)} %all_to_all.31, bf16[576,256]{1,0:T(8,128)(2,1)} %bitcast.62, bf16[576,256]{1,0:T(8,128)(2,1)} %bitcast.63, bf16[576,512]{1,0:T(8,128)(2,1)} %bitcast.59), kind=kOutput, calls=%fused_computation | convolution fusion | flops 22413312 | bytes 1263616 | tf_op jit(solution)/shard_map/dot_general | solution.py:72
  19.4 0.0 copy-start.3
  19.4 36.5 %all-reduce = bf16[16,1024]{1,0:T(8,128)(2,1)S(1)} all-reduce(f32[16,1024]{1,0:T(8,128)S(1)} %fusion), channel_id=2, replica_groups=mesh['dp'=8,'mp'=4] {'dp'}, use_global_device_ids=true, to_apply=%region_1.0.clone | all-reduce | flops 16384 | bytes 98304
  55.9 5.1 %all_gather.14 = bf16[2,1024]{1,0:T(2,128)(2,1)S(1)} all-gather(bf16[2,256]{1,0:T(2,128)(2,1)S(1)} %get-tuple-element.14), channel_id=1, replica_groups=mesh['dp'=8,'mp'=4] {'mp'}, dimensions={1}, use_global_device_ids=true | all-gather | bytes 5120 | tf_op jit(solution)/shard_map/all_gather | solution.py:86
  61.0 0.6 copy.46
  61.6 5.1 %all_gather.13 = bf16[2,1024]{1,0:T(2,128)(2,1)S(1)} all-gather(bf16[2,256]{1,0:T(2,128)(2,1)S(1)} %get-tuple-element.15), channel_id=1, replica_groups=mesh['dp'=8,'mp'=4] {'mp'}, dimensions={1}, use_global_device_ids=true | all-gather | bytes 5120 | tf_op jit(solution)/shard_map/all_gather | solution.py:85
  66.7 5.2 %all_gather.12 = bf16[2,2048]{1,0:T(2,128)(2,1)S(1)} all-gather(bf16[2,512]{1,0:T(2,128)(2,1)S(1)} %slice.31), channel_id=1, replica_groups=mesh['dp'=8,'mp'=4] {'mp'}, dimensions={1}, use_global_device_ids=true | all-gather | bytes 10240 | tf_op jit(solution)/shard_map/all_gather | solution.py:84
  71.9 0.1 subtract_convert_fusion
  71.9 0.1 multiply_subtract_fusion
  72.0 0.1 maximum_bitcast_fusion
  72.1 0.1 fusion.17
  72.2 0.1 fusion.21
  72.3 0.0 copy-done.2
  72.3 0.5 fusion.30
  72.8 7.2 %pmax.7 = f32[2,8,2]{2,1,0:T(8,128)S(1)} all-reduce(f32[2,8,2]{2,1,0:T(8,128)S(1)} %get-tuple-element.20), channel_id=1, replica_groups=mesh['dp'=8,'mp'=4] {'mp'}, use_global_device_ids=true, to_apply=%region_3.4 | all-reduce | flops 32 | bytes 256 | tf_op jit(solution)/shard_map/pmax | solution.py:115
  80.0 0.2 fusion.23
  80.2 0.0 copy-done.3
  80.2 0.3 convolution_multiply_fusion
  80.5 10.3 %all-reduce.1 = (f32[2,8,2,128]{3,2,1,0:T(2,128)S(1)}, f32[2,8,2]{2,1,0:T(8,128)S(1)}) all-reduce(f32[2,8,2,128]{3,2,1,0:T(2,128)S(1)} %convolution_multiply_fusion, f32[2,8,2]{2,1,0:T(8,128)S(1)} %get-tuple-element.8), channel_id=1, replica_groups=mesh['dp'=8,'mp'=4] {'mp'}, use_global_device_ids=true, to_apply=%region_4.5 | all-reduce | flops 4128 | bytes 33024 | tf_op jit(solution)/shard_map/psum | solution.py:117
  90.9 0.1 fusion.18
  91.0 0.0 copy-start.1
  91.1 26.1 %all-gather = bf16[8,2,512]{2,1,0:T(2,128)(2,1)S(1)} all-gather(bf16[1,2,512]{2,1,0:T(2,128)(2,1)S(1)} %dynamic-slice_bitcast_fusion), channel_id=1, replica_groups=mesh['dp'=8,'mp'=4] {'dp'}, dimensions={0}, use_global_device_ids=true | all-gather | bytes 18432 | tf_op jit(solution)/shard_map/all_gather | solution.py:141
  117.2 0.0 copy-done
  117.2 0.3 fusion.9
  117.5 11.2 %psum.23 = f32[8,2,576]{2,1,0:T(2,128)} all-reduce(f32[8,2,576]{2,1,0:T(2,128)S(1)} %all_to_all.32), channel_id=1, replica_groups=mesh['dp'=8,'mp'=4] {'mp'}, use_global_device_ids=true, to_apply=%region_7.8 | all-reduce | flops 9216 | bytes 73728 | tf_op jit(solution)/shard_map/psum | solution.py:145
  128.7 3.3 %all-to-all-start.1 = ((f32[8,2,576]{2,1,0:T(2,128)}), f32[8,2,576]{2,1,0:T(2,128)S(1)}, u32[]{:S(2)}, u32[]{:S(2)}) async-start(f32[8,2,576]{2,1,0:T(2,128)} %psum.23), calls=%async_computation.1 | async-start | bytes 81920 | tf_op jit(solution)/shard_map/all_to_all | solution.py:146
  132.0 0.7 pad_maximum_fusion
  132.7 6.0 %all-to-all-done.1 = f32[8,2,576]{2,1,0:T(2,128)S(1)} async-done(((f32[8,2,576]{2,1,0:T(2,128)}), f32[8,2,576]{2,1,0:T(2,128)S(1)}, u32[]{:S(2)}, u32[]{:S(2)}) %all-to-all-start.1) | async-done | bytes 36896 | tf_op jit(solution)/shard_map/all_to_all | solution.py:146
  138.7 0.2 multiply_reduce_fusion
  138.9 0.1 all_to_all.35
  139.0 0.0 copy-done.1
  139.0 0.7 fusion.16
  (21 shorter events, 0.2 us)
Async XLA Ops:
  0.6 116.6 %copy-start = (bf16[1,512,576]{1,2,0:T(8,128)(2,1)S(1)}, bf16[1,512,576]{1,2,0:T(8,128)(2,1)}, u32[]{:S(2)}) copy-start(bf16[1,512,576]{1,2,0:T(8,128)(2,1)} %param.17) | copy-start | bytes 1769476
  3.9 13.9 %all-to-all-start = ((bf16[2,8,576]{2,0,1:T(2,128)(2,1)}), bf16[2,8,576]{2,0,1:T(2,128)(2,1)S(1)}, u32[]{:S(2)}, u32[]{:S(2)}) async-start(bf16[2,8,576]{2,0,1:T(2,128)(2,1)} %copy.21), calls=%async_computation | async-start | bytes 40960 | tf_op jit(solution)/shard_map/all_to_all | solution.py:65
  17.8 54.5 %copy-start.2 = (bf16[1,2,128,8,128]{4,3,2,1,0:T(8,128)(2,1)S(1)}, bf16[1,2,128,8,128]{4,3,2,1,0:T(8,128)(2,1)}, u32[]{:S(2)}) copy-start(bf16[1,2,128,8,128]{4,3,2,1,0:T(8,128)(2,1)} %param.18) | copy-start | bytes 1572868
  19.4 60.8 %copy-start.3 = (bf16[1,2,128,8,128]{4,3,2,1,0:T(8,128)(2,1)S(1)}, bf16[1,2,128,8,128]{4,3,2,1,0:T(8,128)(2,1)}, u32[]{:S(2)}) copy-start(bf16[1,2,128,8,128]{4,3,2,1,0:T(8,128)(2,1)} %param.19) | copy-start | bytes 1572868
  91.0 48.0 %copy-start.1 = (bf16[2,4608]{1,0:T(2,128)(2,1)S(1)}, bf16[2,4608]{1,0:T(2,128)(2,1)}, u32[]{:S(2)}) copy-start(bf16[2,4608]{1,0:T(2,128)(2,1)} %param.11) | copy-start | bytes 55300
  128.7 10.0 %all-to-all-start.1 = ((f32[8,2,576]{2,1,0:T(2,128)}), f32[8,2,576]{2,1,0:T(2,128)S(1)}, u32[]{:S(2)}, u32[]{:S(2)}) async-start(f32[8,2,576]{2,1,0:T(2,128)} %psum.23), calls=%async_computation.1 | async-start | bytes 81920 | tf_op jit(solution)/shard_map/all_to_all | solution.py:146
where the time goes:
time: 140 us
  blocking collectives  107 us (76%)
  starting transfers between devices  10.6 us (8%)
  other arithmetic  7.74 us (6%)
  waiting for transfers between devices  7.67 us (5%)
  local copies, waits for them, and re-layouts  2.81 us (2%)
  matrix products  2.7 us (2%)
  between operations  1.49 us (1%)
    unnamed x1, blocking collectives  36.5 us
    all_gather x1, blocking collectives, on_device(): all_rows = lax.all_gather(attended_local, 'dp', axis=0, tiled=True)  26.1 us
    psum x1, blocking collectives, on_device(): partial_cols = lax.psum(partial_cols, 'mp')  11.2 us
    psum x1, blocking collectives, on_device(): lax.psum((sums_exp * rescale, accumulated * rescale[..., None]), 'mp')  10.3 us
    all_to_all x1, starting transfers between devices, on_device(): lax.all_to_all(normed, 'dp', split_axis=1, concat_axis=0, tiled=True)  7.28 us
    pmax x1, blocking collectives, on_device(): global_peak = lax.pmax(peaks, 'mp')  7.24 us
    all_to_all x1, waiting for transfers between devices, on_device(): lax.all_to_all(partial_cols, 'dp', split_axis=0, concat_axis=1, tiled=True)  6.01 us
    all_gather x1, blocking collectives, on_device(): lax.all_gather(rounded[0], 'mp', axis=1, tiled=True)  5.18 us
  transfers between devices with their start and end apart: 2, of which 2 were waited for; matrix products, arithmetic and copies ran while one was open for 4% of the time, Pallas kernels for 0%

commit v1 on v0

--- a/solution.py
+++ b/solution.py
@@ -142,7 +142,7 @@
         partial_cols = jnp.dot(
             all_rows, out_weight[layer_index], preferred_element_type=jnp.float32
         )
-        partial_cols = lax.psum(partial_cols, "mp")
+        partial_cols = jnp.sum(lax.all_gather(partial_cols, "mp"), axis=0)
         projected = lax.all_to_all(partial_cols, "dp", split_axis=0, concat_axis=1, tiled=True)
         hidden = (hidden.astype(jnp.float32) + rms_scale(projected, post_gain[layer_index])).astype(
             jnp.bfloat16

time: 140 us -> 135 us (0.964)
  blocking collectives: 107 us -> 101 us
    psum x1 -> x0, blocking collectives: 11.2 us -> none  [on_device(): partial_cols = lax.psum(partial_cols, 'mp')]
    all_gather x0 -> x1, blocking collectives: none -> 5.51 us  [on_device(): partial_cols = jnp.sum(lax.all_gather(partial_cols, 'mp'), axis=0)]
where the time goes in v1:
time: 135 us; the launch traced here: 134 us
  blocking collectives  101 us (75%)
  starting transfers between devices  10.6 us (8%)
  other arithmetic  7.76 us (6%)
  waiting for transfers between devices  7.09 us (5%)
  local copies, waits for them, and re-layouts  3.41 us (3%)
  matrix products  2.69 us (2%)
  between operations  1.46 us (1%)
    unnamed x1, blocking collectives  36.5 us
    all_gather x1, blocking collectives, on_device(): all_rows = lax.all_gather(attended_local, 'dp', axis=0, tiled=True)  26.1 us
    psum x1, blocking collectives, on_device(): lax.psum((sums_exp * rescale, accumulated * rescale[..., None]), 'mp')  10.6 us
    all_to_all x1, starting transfers between devices, on_device(): lax.all_to_all(normed, 'dp', split_axis=1, concat_axis=0, tiled=True)  7.28 us
    pmax x1, blocking collectives, on_device(): global_peak = lax.pmax(peaks, 'mp')  7.23 us
    all_gather x1, blocking collectives, on_device(): partial_cols = jnp.sum(lax.all_gather(partial_cols, 'mp'), axis=0)  5.51 us
    all_to_all x1, waiting for transfers between devices, on_device(): lax.all_to_all(partial_cols, 'dp', split_axis=0, concat_axis=1, tiled=True)  5.41 us
    all_gather x1, blocking collectives, on_device(): lax.all_gather(rounded[0], 'mp', axis=1, tiled=True)  5.19 us
  transfers between devices with their start and end apart: 2, of which 2 were waited for; matrix products, arithmetic and copies ran while one was open for 4% of the time, Pallas kernels for 0%

profile of v1, /device:TPU:0, one launch (start us, length us, event | category | flops | bytes accessed | tf_op | source)
XLA Modules:
  0.0 134.3 jit_solution(6440620235763371901)
XLA Ops:
  0.6 0.0 copy-start
  0.6 0.9 fusion.13
  1.6 0.8 reduce.1
  2.4 0.8 fusion.15
  3.2 0.1 all_to_all.28
  3.3 0.6 copy.23
  3.9 7.3 %all-to-all-start = ((bf16[2,8,576]{2,0,1:T(2,128)(2,1)}), bf16[2,8,576]{2,0,1:T(2,128)(2,1)S(1)}, u32[]{:S(2)}, u32[]{:S(2)}) async-start(bf16[2,8,576]{2,0,1:T(2,128)(2,1)} %copy.23), calls=%async_computation | async-start | bytes 40960 | tf_op jit(solution)/shard_map/all_to_all | solution.py:65
  11.2 0.7 broadcast_add_fusion
  11.9 0.7 compare_bitcast_fusion
  12.6 0.1 multiply_cosine_fusion
  12.7 0.7 or_and_fusion
  13.4 0.8 reduce.2
  14.2 1.2 dynamic-slice
  16.1 1.7 %all-to-all-done = bf16[2,8,576]{2,0,1:T(2,128)(2,1)S(1)} async-done(((bf16[2,8,576]{2,0,1:T(2,128)(2,1)}), bf16[2,8,576]{2,0,1:T(2,128)(2,1)S(1)}, u32[]{:S(2)}, u32[]{:S(2)}) %all-to-all-start) | async-done | bytes 18464 | tf_op jit(solution)/shard_map/all_to_all | solution.py:65
  17.8 0.0 copy-start.2
  17.8 1.6 %fusion = f32[16,1024]{1,0:T(8,128)S(1)} fusion(bf16[16,576]{1,0:T(8,128)(2,1)S(1)} %all_to_all.31, bf16[576,256]{1,0:T(8,128)(2,1)} %bitcast.64, bf16[576,256]{1,0:T(8,128)(2,1)} %bitcast.65, bf16[576,512]{1,0:T(8,128)(2,1)} %bitcast.61), kind=kOutput, calls=%fused_computation | convolution fusion | flops 22413312 | bytes 1263616 | tf_op jit(solution)/shard_map/dot_general | solution.py:72
  19.4 0.0 copy-start.3
  19.4 36.5 %all-reduce = bf16[16,1024]{1,0:T(8,128)(2,1)S(1)} all-reduce(f32[16,1024]{1,0:T(8,128)S(1)} %fusion), channel_id=3, replica_groups=mesh['dp'=8,'mp'=4] {'dp'}, use_global_device_ids=true, to_apply=%region_1.0.clone | all-reduce | flops 16384 | bytes 98304
  55.9 5.2 %all_gather.18 = bf16[2,2048]{1,0:T(2,128)(2,1)S(1)} all-gather(bf16[2,512]{1,0:T(2,128)(2,1)S(1)} %slice.31), channel_id=1, replica_groups=mesh['dp'=8,'mp'=4] {'mp'}, dimensions={1}, use_global_device_ids=true | all-gather | bytes 10240 | tf_op jit(solution)/shard_map/all_gather | solution.py:84
  61.1 0.1 multiply_subtract_fusion
  61.2 0.1 fusion.17
  61.3 0.0 copy-done.2
  61.3 0.4 fusion.30
  61.8 7.2 %pmax.7 = f32[2,8,2]{2,1,0:T(8,128)S(1)} all-reduce(f32[2,8,2]{2,1,0:T(8,128)S(1)} %get-tuple-element.20), channel_id=1, replica_groups=mesh['dp'=8,'mp'=4] {'mp'}, use_global_device_ids=true, to_apply=%region_3.4 | all-reduce | flops 32 | bytes 256 | tf_op jit(solution)/shard_map/pmax | solution.py:115
  69.0 0.2 fusion.23
  69.2 5.1 %all_gather.19 = bf16[2,1024]{1,0:T(2,128)(2,1)S(1)} all-gather(bf16[2,256]{1,0:T(2,128)(2,1)S(1)} %get-tuple-element.15), channel_id=1, replica_groups=mesh['dp'=8,'mp'=4] {'mp'}, dimensions={1}, use_global_device_ids=true | all-gather | bytes 5120 | tf_op jit(solution)/shard_map/all_gather | solution.py:85
  74.3 0.1 subtract_convert_fusion
  74.3 0.1 maximum_bitcast_fusion
  74.4 0.1 fusion.21
  74.5 5.1 %all_gather.20 = bf16[2,1024]{1,0:T(2,128)(2,1)S(1)} all-gather(bf16[2,256]{1,0:T(2,128)(2,1)S(1)} %get-tuple-element.14), channel_id=1, replica_groups=mesh['dp'=8,'mp'=4] {'mp'}, dimensions={1}, use_global_device_ids=true | all-gather | bytes 5120 | tf_op jit(solution)/shard_map/all_gather | solution.py:86
  79.6 0.0 copy-done.3
  79.6 0.3 convolution_multiply_fusion
  79.9 10.6 %all-reduce.1 = (f32[2,8,2,128]{3,2,1,0:T(2,128)S(1)}, f32[2,8,2]{2,1,0:T(8,128)S(1)}) all-reduce(f32[2,8,2,128]{3,2,1,0:T(2,128)S(1)} %convolution_multiply_fusion, f32[2,8,2]{2,1,0:T(8,128)S(1)} %get-tuple-element.8), channel_id=1, replica_groups=mesh['dp'=8,'mp'=4] {'mp'}, use_global_device_ids=true, to_apply=%region_4.5 | all-reduce | flops 4128 | bytes 33024 | tf_op jit(solution)/shard_map/psum | solution.py:117
  90.5 0.1 fusion.18
  90.7 26.1 %all-gather.1 = bf16[8,2,512]{2,1,0:T(2,128)(2,1)S(1)} all-gather(bf16[1,2,512]{2,1,0:T(2,128)(2,1)S(1)} %dynamic-slice_bitcast_fusion), channel_id=1, replica_groups=mesh['dp'=8,'mp'=4] {'dp'}, dimensions={0}, use_global_device_ids=true | all-gather | bytes 18432 | tf_op jit(solution)/shard_map/all_gather | solution.py:141
  116.8 0.0 copy-done
  116.8 0.0 copy-start.1
  116.9 0.3 fusion.9
  117.1 5.5 %all-gather = f32[64,576]{1,0:T(8,128)S(1)} all-gather(f32[16,576]{1,0:T(8,128)S(1)} %fusion.9), channel_id=2, replica_groups=mesh['dp'=8,'mp'=4] {'mp'}, dimensions={0}, use_global_device_ids=true | all-gather | bytes 184320 | tf_op jit(solution)/shard_map/all_gather | solution.py:145
  122.6 0.6 all_to_all.32
  123.3 3.3 %all-to-all-start.1 = ((f32[8,2,576]{2,1,0:T(2,128)}), f32[8,2,576]{2,1,0:T(2,128)S(1)}, u32[]{:S(2)}, u32[]{:S(2)}) async-start(f32[8,2,576]{2,1,0:T(2,128)} %all_to_all.32), calls=%async_computation.1 | async-start | bytes 81920 | tf_op jit(solution)/shard_map/all_to_all | solution.py:146
  126.6 0.6 copy.48
  127.2 0.7 pad_maximum_fusion
  127.9 5.4 %all-to-all-done.1 = f32[8,2,576]{2,1,0:T(2,128)S(1)} async-done(((f32[8,2,576]{2,1,0:T(2,128)}), f32[8,2,576]{2,1,0:T(2,128)S(1)}, u32[]{:S(2)}, u32[]{:S(2)}) %all-to-all-start.1) | async-done | bytes 36896 | tf_op jit(solution)/shard_map/all_to_all | solution.py:146
  133.3 0.1 all_to_all.35
  133.4 0.2 multiply_reduce_fusion
  133.6 0.0 copy-done.1
  133.6 0.7 fusion.16
  (21 shorter events, 0.2 us)
Async XLA Ops:
  0.6 116.2 %copy-start = (bf16[1,512,576]{1,2,0:T(8,128)(2,1)S(1)}, bf16[1,512,576]{1,2,0:T(8,128)(2,1)}, u32[]{:S(2)}) copy-start(bf16[1,512,576]{1,2,0:T(8,128)(2,1)} %param.17) | copy-start | bytes 1769476
  3.9 13.9 %all-to-all-start = ((bf16[2,8,576]{2,0,1:T(2,128)(2,1)}), bf16[2,8,576]{2,0,1:T(2,128)(2,1)S(1)}, u32[]{:S(2)}, u32[]{:S(2)}) async-start(bf16[2,8,576]{2,0,1:T(2,128)(2,1)} %copy.23), calls=%async_computation | async-start | bytes 40960 | tf_op jit(solution)/shard_map/all_to_all | solution.py:65
  17.8 43.5 %copy-start.2 = (bf16[1,2,128,8,128]{4,3,2,1,0:T(8,128)(2,1)S(1)}, bf16[1,2,128,8,128]{4,3,2,1,0:T(8,128)(2,1)}, u32[]{:S(2)}) copy-start(bf16[1,2,128,8,128]{4,3,2,1,0:T(8,128)(2,1)} %param.18) | copy-start | bytes 1572868
  19.4 60.2 %copy-start.3 = (bf16[1,2,128,8,128]{4,3,2,1,0:T(8,128)(2,1)S(1)}, bf16[1,2,128,8,128]{4,3,2,1,0:T(8,128)(2,1)}, u32[]{:S(2)}) copy-start(bf16[1,2,128,8,128]{4,3,2,1,0:T(8,128)(2,1)} %param.19) | copy-start | bytes 1572868
  116.8 16.7 %copy-start.1 = (bf16[2,4608]{1,0:T(2,128)(2,1)S(1)}, bf16[2,4608]{1,0:T(2,128)(2,1)}, u32[]{:S(2)}) copy-start(bf16[2,4608]{1,0:T(2,128)(2,1)} %param.11) | copy-start | bytes 55300
  123.3 10.0 %all-to-all-start.1 = ((f32[8,2,576]{2,1,0:T(2,128)}), f32[8,2,576]{2,1,0:T(2,128)S(1)}, u32[]{:S(2)}, u32[]{:S(2)}) async-start(f32[8,2,576]{2,1,0:T(2,128)} %all_to_all.32), calls=%async_computation.1 | async-start | bytes 81920 | tf_op jit(solution)/shard_map/all_to_all | solution.py:146
